TPU v7x, 32 devices: a whole 2x2x4 slice. The times are simulated.
32 devices in a mesh: dp: 4 (over z), tensor: 8 (over y, x, core).
Axes of the slice: x: 2, y: 2, z: 4, core: 2. Of those that a mesh axis runs over, the one named last changes fastest.
Arguments:
- layer_input: bfloat16 [16384, 2048], P(('dp', 'tensor')), may hold values from -20 to 20
- gain_attn: float32 [2048], replicated, may hold values from 0.25 to 1.75
- w_query: bfloat16 [2048, 2048], P(None, 'tensor'), may hold values from -0.125 to 0.125
- w_key: bfloat16 [2048, 2048], P(None, 'tensor'), may hold values from -0.125 to 0.125
- w_value: bfloat16 [2048, 2048], P(None, 'tensor'), may hold values from -0.125 to 0.125
- w_out: bfloat16 [2048, 2048], P('tensor'), may hold values from -1 to 1
- gain_mlp: float32 [2048], replicated, may hold values from 0.25 to 1.75
- w_gate: bfloat16 [2048, 8192], P(None, 'tensor'), may hold values from -0.125 to 0.125
- w_up: bfloat16 [2048, 8192], P(None, 'tensor'), may hold values from -0.125 to 0.125
- w_down: bfloat16 [8192, 2048], P('tensor'), may hold values from -0.0625 to 0.0625
- segment_ids: int32 [8, 2048], P('dp'), may hold values from 0 to 31, as said below
- positions: int32 [8, 2048], P('dp'), may hold values from 0 to 2047, as said below
- out_grad: bfloat16 [16384, 2048], P(('dp', 'tensor')), may hold values from -6 to 6
Outputs:
- layer_out: bfloat16 [16384, 2048], P(('dp', 'tensor'))
- input_grad: float32 [16384, 2048], P(('dp', 'tensor'))
- grad_gain_attn: float32 [2048], P('tensor')
- grad_w_query: float32 [2048, 2048], P(None, 'tensor')
- grad_w_key: float32 [2048, 2048], P(None, 'tensor')
- grad_w_value: float32 [2048, 2048], P(None, 'tensor')
- grad_w_out: float32 [2048, 2048], P('tensor')
- grad_gain_mlp: float32 [2048], P('tensor')
- grad_w_gate: float32 [2048, 8192], P(None, 'tensor')
- grad_w_up: float32 [2048, 8192], P(None, 'tensor')
- grad_w_down: float32 [8192, 2048], P('tensor')
Inputs may be any that keep to these rules, and one draw needn't show every extreme that they name: `segment_ids`: within each row the document number is 0 at the first token and rises by 0 or 1 from one token to the next; a row holds 1 to 32 documents; the first row of the batch is one document and the last row holds 32. `positions`: A position is 0 where a row begins or the document number changes, else one more than the position before.
All inputs are finite; a program needn't handle non-finite values.
Results may differ from a plain program's by a relative error of at most 0.024.
Values may be sent and summed in bfloat16 or wider, within the bound.
A program may use at most 320 MiB of HBM per device.

v0:
```python
import jax
import jax.numpy as jnp
from jax import lax
from jax.sharding import PartitionSpec as P

HD = 64
rope_theta = 130000.0
norm_eps = 1e-05


def rotary_tables(position_list, head_size):
    half_dim = head_size // 2
    frequency = rope_theta ** (-(jnp.arange(half_dim, dtype=jnp.float32) * 2.0 / head_size))
    angles = position_list.astype(jnp.float32)[:, None] * frequency[None, :]
    cosine_table = jnp.concatenate([jnp.cos(angles), jnp.cos(angles)], axis=-1)[:, None, :]
    sine_table = jnp.concatenate([jnp.sin(angles), jnp.sin(angles)], axis=-1)[:, None, :]
    return (cosine_table, sine_table)


def rotate(inputs, cosine_table, sine_table):
    half_dim = inputs.shape[-1] // 2
    turned = jnp.concatenate([-inputs[..., half_dim:], inputs[..., :half_dim]], axis=-1)
    return inputs * cosine_table + turned * sine_table


def rotate_back(grad_in, cosine_table, sine_table):
    half_dim = grad_in.shape[-1] // 2
    scaled = grad_in * sine_table
    turned = jnp.concatenate([scaled[..., half_dim:], -scaled[..., :half_dim]], axis=-1)
    return grad_in * cosine_table + turned


def normalize(row_values):
    inverse = lax.rsqrt(jnp.mean(row_values * row_values, axis=-1, keepdims=True) + norm_eps)
    return (row_values * inverse, inverse)


def norm_back(grad_in, gain_vec, unit_rows, inverse):
    scaled = grad_in * gain_vec
    return inverse * (scaled - unit_rows * jnp.mean(scaled * unit_rows, axis=-1, keepdims=True))


def project_attend(gathered, joined_w, position_ids, hidden_w):
    token_count = gathered.shape[0]
    local_heads = hidden_w // HD
    projected = jnp.dot(gathered, joined_w, preferred_element_type=jnp.float32)
    cosine_table, sine_table = rotary_tables(position_ids.reshape(-1), HD)
    queries = rotate(
        projected[:, :hidden_w].reshape(token_count, local_heads, HD), cosine_table, sine_table
    ).astype(jnp.bfloat16)
    key_heads = rotate(
        projected[:, hidden_w : 2 * hidden_w].reshape(token_count, local_heads, HD),
        cosine_table,
        sine_table,
    ).astype(jnp.bfloat16)
    value_heads = (
        projected[:, 2 * hidden_w :].reshape(token_count, local_heads, HD).astype(jnp.bfloat16)
    )
    return (queries, key_heads, value_heads, cosine_table, sine_table)


def block_mask(segment_row, first_row, block_len):
    q_index = first_row + jnp.arange(block_len, dtype=jnp.int32)
    k_index = jnp.arange(segment_row.shape[0], dtype=jnp.int32)
    seg_query = lax.dynamic_slice_in_dim(segment_row, first_row, block_len)
    return (seg_query[:, None] == segment_row[None, :]) & (k_index[None, :] <= q_index[:, None])


def block_scores(query_block, key_row, allowed):
    scores = jnp.einsum(
        "qhd,khd->hqk", query_block, key_row, preferred_element_type=jnp.float32
    ) * HD ** (-0.5)
    return jnp.where(allowed[None], scores, -1e30)


def attend_forward(queries, key_heads, value_heads, segment_ids):
    row_count, length = segment_ids.shape
    local_heads = queries.shape[1]
    block_len = min(512, length)
    per_row = length // block_len
    query_rows = queries.reshape(row_count, length, local_heads, HD)
    key_rows = key_heads.reshape(row_count, length, local_heads, HD)
    value_rows = value_heads.reshape(row_count, length, local_heads, HD)

    def one_block(block_index):
        row_index = block_index // per_row
        first_row = block_index % per_row * block_len
        query_block = lax.dynamic_slice_in_dim(query_rows[row_index], first_row, block_len, 0)
        scores = block_scores(
            query_block,
            key_rows[row_index],
            block_mask(segment_ids[row_index], first_row, block_len),
        )
        row_max = jnp.max(scores, axis=-1, keepdims=True)
        exp_scores = jnp.exp(scores - row_max)
        exp_total = jnp.sum(exp_scores, axis=-1, keepdims=True)
        probabilities = (exp_scores / exp_total).astype(jnp.bfloat16)
        mixed = jnp.einsum(
            "hqk,khd->qhd", probabilities, value_rows[row_index], preferred_element_type=jnp.float32
        )
        return (mixed.astype(jnp.bfloat16), (row_max + jnp.log(exp_total))[..., 0])

    mixed_all, log_total = lax.map(one_block, jnp.arange(row_count * per_row, dtype=jnp.int32))
    return (mixed_all.reshape(row_count * length, local_heads * HD), log_total)


def attend_backward(queries, key_heads, value_heads, d_mixed, log_total, segment_ids):
    row_count, length = segment_ids.shape
    local_heads = queries.shape[1]
    block_len = min(512, length)
    per_row = length // block_len
    scale_factor = HD ** (-0.5)
    query_rows = queries.reshape(row_count, length, local_heads, HD)
    key_rows = key_heads.reshape(row_count, length, local_heads, HD)
    value_rows = value_heads.reshape(row_count, length, local_heads, HD)
    grad_rows = d_mixed.reshape(row_count, length, local_heads, HD)

    def one_row(row_index):
        query_row = query_rows[row_index]
        key_row = key_rows[row_index]
        value_row = value_rows[row_index]
        grad_row = grad_rows[row_index]
        segment_row = segment_ids[row_index]

        def one_step(running, block_number):
            d_key_acc, d_value_acc = running
            first_row = block_number * block_len
            query_block = lax.dynamic_slice_in_dim(query_row, first_row, block_len, 0)
            grad_block = lax.dynamic_slice_in_dim(grad_row, first_row, block_len, 0)
            scores = block_scores(
                query_block, key_row, block_mask(segment_row, first_row, block_len)
            )
            level_block = log_total[row_index * per_row + block_number][:, :, None]
            probabilities = jnp.exp(scores - level_block)
            d_probs = jnp.einsum(
                "qhd,khd->hqk", grad_block, value_row, preferred_element_type=jnp.float32
            )
            centre = jnp.sum(d_probs * probabilities, axis=-1, keepdims=True)
            d_scores = (probabilities * (d_probs - centre)).astype(jnp.bfloat16)
            d_query_block = (
                jnp.einsum("hqk,khd->qhd", d_scores, key_row, preferred_element_type=jnp.float32)
                * scale_factor
            )
            d_key_acc = (
                d_key_acc
                + jnp.einsum(
                    "hqk,qhd->khd", d_scores, query_block, preferred_element_type=jnp.float32
                )
                * scale_factor
            )
            d_value_acc = d_value_acc + jnp.einsum(
                "hqk,qhd->khd",
                probabilities.astype(jnp.bfloat16),
                grad_block,
                preferred_element_type=jnp.float32,
            )
            return ((d_key_acc, d_value_acc), d_query_block)

        zero_rows = jnp.zeros((length, local_heads, HD), jnp.float32)
        (d_key_row, d_value_row), d_query_blocks = lax.scan(
            one_step, (zero_rows, zero_rows), jnp.arange(per_row, dtype=jnp.int32)
        )
        return (d_query_blocks.reshape(length, local_heads, HD), d_key_row, d_value_row)

    d_queries, d_keys, d_values = lax.map(one_row, jnp.arange(row_count, dtype=jnp.int32))
    token_count = row_count * length
    return (
        d_queries.reshape(token_count, local_heads, HD),
        d_keys.reshape(token_count, local_heads, HD),
        d_values.reshape(token_count, local_heads, HD),
    )


def mlp_hidden(gathered, both_w, ff_local):
    projected = jnp.dot(gathered, both_w, preferred_element_type=jnp.float32)
    gate_pre = projected[:, :ff_local]
    up_pre = projected[:, ff_local:]
    hidden = (jax.nn.silu(gate_pre) * up_pre).astype(jnp.bfloat16)
    return (gate_pre, up_pre, hidden)


def local(
    layer_input,
    gain_attn,
    w_query,
    w_key,
    w_value,
    w_out,
    gain_mlp,
    w_gate,
    w_up,
    w_down,
    segment_ids,
    positions,
    out_grad,
):
    shard_rows, width = layer_input.shape
    tensor_size = lax.axis_size("tensor")
    hidden_w = w_query.shape[1]
    ff_local = w_gate.shape[1]
    joined_w = jnp.concatenate([w_query, w_key, w_value], axis=1)
    both_w = jnp.concatenate([w_gate, w_up], axis=1)
    inputs = layer_input.astype(jnp.float32)
    unit_one, inverse_one = normalize(inputs)
    normed_one = (unit_one * gain_attn).astype(jnp.bfloat16)
    gathered_one = lax.all_gather(normed_one, "tensor", axis=0, tiled=True)
    queries, key_heads, value_heads, cosine_table, sine_table = project_attend(
        gathered_one, joined_w, positions, hidden_w
    )
    attended, log_total = attend_forward(queries, key_heads, value_heads, segment_ids)
    residual = inputs + lax.psum_scatter(
        jnp.dot(attended, w_out, preferred_element_type=jnp.float32).astype(jnp.bfloat16),
        "tensor",
        scatter_dimension=0,
        tiled=True,
    ).astype(jnp.float32)
    unit_two, inverse_two = normalize(residual)
    normed_two = (unit_two * gain_mlp).astype(jnp.bfloat16)
    gathered_two = lax.all_gather(normed_two, "tensor", axis=0, tiled=True)
    gate_pre, up_pre, hidden = mlp_hidden(gathered_two, both_w, ff_local)
    layer_out = (
        residual
        + lax.psum_scatter(
            jnp.dot(hidden, w_down, preferred_element_type=jnp.float32).astype(jnp.bfloat16),
            "tensor",
            scatter_dimension=0,
            tiled=True,
        ).astype(jnp.float32)
    ).astype(jnp.bfloat16)
    token_count = gathered_two.shape[0]
    shard_piece = lax.all_gather(out_grad, "tensor", axis=0, tiled=True)
    d_down = lax.dot_general(
        hidden, shard_piece, (((0,), (0,)), ((), ())), preferred_element_type=jnp.float32
    )
    part_rows = lax.dot_general(
        shard_piece, w_down, (((1,), (1,)), ((), ())), preferred_element_type=jnp.float32
    )
    d_hidden = part_rows
    sigmoid_gate = jax.nn.sigmoid(gate_pre)
    d_up = d_hidden * (gate_pre * sigmoid_gate)
    d_gate = d_hidden * up_pre * sigmoid_gate * (1.0 + gate_pre * (1.0 - sigmoid_gate))
    d_both = jnp.concatenate([d_gate, d_up], axis=1).astype(jnp.bfloat16)
    grad_both = lax.dot_general(
        gathered_two, d_both, (((0,), (0,)), ((), ())), preferred_element_type=jnp.float32
    )
    rows_here = d_both
    d_normed_two = lax.psum_scatter(
        lax.dot_general(
            rows_here, both_w, (((1,), (1,)), ((), ())), preferred_element_type=jnp.float32
        ).astype(jnp.bfloat16),
        "tensor",
        scatter_dimension=0,
        tiled=True,
    ).astype(jnp.float32)
    gain_two_part = jnp.sum(d_normed_two * unit_two, axis=0)
    d_residual = out_grad.astype(jnp.float32) + norm_back(
        d_normed_two, gain_mlp, unit_two, inverse_two
    )
    d_attn = d_residual.astype(jnp.bfloat16)
    shard_piece = lax.all_gather(d_attn, "tensor", axis=0, tiled=True)
    d_outw = lax.dot_general(
        attended, shard_piece, (((0,), (0,)), ((), ())), preferred_element_type=jnp.float32
    )
    part_rows = lax.dot_general(
        shard_piece, w_out, (((1,), (1,)), ((), ())), preferred_element_type=jnp.float32
    )
    d_queries, d_keys, d_values = attend_backward(
        queries, key_heads, value_heads, part_rows.astype(jnp.bfloat16), log_total, segment_ids
    )
    d_projected = jnp.concatenate(
        [
            rotate_back(d_queries, cosine_table, sine_table).reshape(token_count, hidden_w),
            rotate_back(d_keys, cosine_table, sine_table).reshape(token_count, hidden_w),
            d_values.reshape(token_count, hidden_w),
        ],
        axis=1,
    ).astype(jnp.bfloat16)
    grad_joined = lax.dot_general(
        gathered_one, d_projected, (((0,), (0,)), ((), ())), preferred_element_type=jnp.float32
    )
    rows_here = d_projected
    d_normed_one = lax.psum_scatter(
        lax.dot_general(
            rows_here, joined_w, (((1,), (1,)), ((), ())), preferred_element_type=jnp.float32
        ).astype(jnp.bfloat16),
        "tensor",
        scatter_dimension=0,
        tiled=True,
    ).astype(jnp.float32)
    gain_one_part = jnp.sum(d_normed_one * unit_one, axis=0)
    input_grad = d_residual + norm_back(d_normed_one, gain_attn, unit_one, inverse_one)
    summed_joined, summed_outw, summed_both, summed_down = (
        lax.psum(grad_joined.astype(jnp.bfloat16), "dp").astype(jnp.float32),
        lax.psum(d_outw.astype(jnp.bfloat16), "dp").astype(jnp.float32),
        lax.psum(grad_both.astype(jnp.bfloat16), "dp").astype(jnp.float32),
        lax.psum(d_down.astype(jnp.bfloat16), "dp").astype(jnp.float32),
    )
    gain_one_all, gain_two_all = lax.psum((gain_one_part, gain_two_part), ("dp", "tensor"))
    gain_piece = width // tensor_size
    gain_start = lax.axis_index("tensor") * gain_piece
    grad_gain_one = lax.dynamic_slice_in_dim(gain_one_all, gain_start, gain_piece)
    grad_gain_two = lax.dynamic_slice_in_dim(gain_two_all, gain_start, gain_piece)
    return (
        layer_out,
        input_grad,
        grad_gain_one,
        summed_joined[:, :hidden_w],
        summed_joined[:, hidden_w : 2 * hidden_w],
        summed_joined[:, 2 * hidden_w :],
        summed_outw,
        grad_gain_two,
        summed_both[:, :ff_local],
        summed_both[:, ff_local:],
        summed_down,
    )


def solution(mesh):
    return jax.shard_map(
        local,
        mesh=mesh,
        in_specs=(
            P(("dp", "tensor"), None),
            P(),
            P(None, "tensor"),
            P(None, "tensor"),
            P(None, "tensor"),
            P("tensor", None),
            P(),
            P(None, "tensor"),
            P(None, "tensor"),
            P("tensor", None),
            P("dp", None),
            P("dp", None),
            P(("dp", "tensor"), None),
        ),
        out_specs=(
            P(("dp", "tensor"), None),
            P(("dp", "tensor"), None),
            P("tensor"),
            P(None, "tensor"),
            P(None, "tensor"),
            P(None, "tensor"),
            P("tensor", None),
            P("tensor"),
            P(None, "tensor"),
            P(None, "tensor"),
            P("tensor", None),
        ),
        check_vma=False,
    )
```

profile of v0, /device:TPU:0, one launch (start us, length us, event | category | flops | bytes accessed | tf_op | source)
XLA Modules:
  0.0 2408.1 jit_solution(8862629533431668547)
XLA Ops:
  27.1 79.2 %all-gather.5.cloned.1.call-done = bf16[4096,2048]{1,0:T(8,128)(2,1)} async-done(((bf16[512,2048]{1,0:T(8,128)(2,1)}), bf16[4096,2048]{1,0:T(8,128)(2,1)}) %all-gather.5.cloned.1.call-update) | async-done | bytes 16777232 | tf_op jit(solution)/shard_map/all_gather | solution.py:206
  106.2 20.4 fusion.84
  194.7 164.5 %while.46 = (s32[]{:T(128)}, bf16[8,512,4,64]{1,3,2,0:T(8,128)(2,1)}, f32[8,4,512]{2,1,0:T(4,128)}, s32[8]{0:T(128)S(1)}, bf16[2,2048,4,64]{1,3,2,0:T(8,128)(2,1...) while((s32[]{:T(128)}, ...), condition=%wide.region_4.5_spmd, body=%wide.region_1.4_spmd.sunk | while | flops 1127348736 | bytes 57248256 | solution.py:103
  375.3 115.8 %reduce-scatter.5.cloned.1.call-done = bf16[512,2048]{1,0:T(8,128)(2,1)} async-done(((bf16[4096,2048]{1,0:T(8,128)(2,1)}), bf16[512,2048]{1,0:T(8,128)(2,1)}) %reduce-scatter.5.cloned.1.call-update) | async-done | bytes 2097168 | tf_op jit(solution)/shard_map/reduce_scatter | solution.py:211
  504.8 81.7 %all-gather.7.cloned.1.call-done = bf16[4096,2048]{1,0:T(8,128)(2,1)} async-done(((bf16[512,2048]{1,0:T(8,128)(2,1)}), bf16[4096,2048]{1,0:T(8,128)(2,1)}) %all-gather.7.cloned.1.call-update) | async-done | bytes 16777232 | tf_op jit(solution)/shard_map/all_gather | solution.py:219
  586.5 44.9 %fusion.85 = f32[4096,2048]{0,1:T(8,128)} fusion(bf16[4096,2048]{1,0:T(8,128)(2,1)} %all-gather.7.cloned.1.call-done, bf16[2048,2048]{1,0:T(8,128)(2,1)} %constant_dynamic-update-slice_fusion.3), kind=kOutput, calls=%fused_computation.157 | convolution fusion | flops 34359738368 | bytes 58720256 | tf_op jit(solution)/shard_map/dot_general | solution.py:175
  631.4 46.6 %all-gather.9.cloned.1.call-done = bf16[4096,2048]{1,0:T(8,128)(2,1)} async-done(((bf16[512,2048]{1,0:T(8,128)(2,1)}), bf16[4096,2048]{1,0:T(8,128)(2,1)}) %all-gather.9.cloned.1.call-update) | async-done | bytes 16777232 | tf_op jit(solution)/shard_map/all_gather | solution.py:231
  678.0 36.1 %multiply_convert_fusion.2 = (bf16[4096,1024]{0,1:T(8,128)(2,1)}, bf16[4096,1024]{0,1:T(8,128)(2,1)}, bf16[4096,1024]{0,1:T(8,128)(2,1)}) fusion(f32[4096,2048]{0,1:T(8,128)} %fusion.85, bf16[4096,2048]{1,0:T(8,128)(2,1)} %all-gather.9.cloned.1.call-done, bf16[1024,2048]{1,0:T(8,128)(2,1)} %param.28), kind=kOutput, calls=%fused_computation.64 | convolution fusion | flops 17242783744 | bytes 79691776 | tf_op jit(solution)/shard_map/dot_general | solution.py:235
  714.1 42.1 %convolution_convert_fusion.3 = bf16[4096,2048]{1,0:T(8,128)(2,1)} fusion(bf16[2048,2048]{1,0:T(8,128)(2,1)} %constant_dynamic-update-slice_fusion.3, bf16[4096,1024]{0,1:T(8,128)(2,1)} %get-tuple-element.527, bf16[4096,1024]{0,1:T(8,128)(2,1)} %get-tuple-element.526), kind=kOutput, calls=%fused_computation.71 | convolution fusion | flops 34401681408 | bytes 41943040 | tf_op jit(solution)/shard_map/dot_general | solution.py:248
  756.5 116.1 %reduce-scatter.9.cloned.1.call-done = bf16[512,2048]{1,0:T(8,128)(2,1)} async-done(((bf16[4096,2048]{1,0:T(8,128)(2,1)}), bf16[512,2048]{1,0:T(8,128)(2,1)}) %reduce-scatter.9.cloned.1.call-update) | async-done | bytes 2097168 | tf_op jit(solution)/shard_map/reduce_scatter | solution.py:247
  885.0 24.7 %convolution_convert_fusion.5 = bf16[1024,2048]{1,0:T(8,128)(2,1)} fusion(bf16[4096,1024]{0,1:T(8,128)(2,1)} %get-tuple-element.528, bf16[4096,2048]{1,0:T(8,128)(2,1)} %all-gather.9.cloned.1.call-done), kind=kOutput, calls=%fused_computation.117 | convolution fusion | flops 17181966336 | bytes 29360128 | tf_op jit(solution)/shard_map/dot_general | solution.py:232
  909.7 45.5 %fusion.47 = bf16[2048,2048]{1,0:T(8,128)(2,1)} fusion(bf16[4096,2048]{1,0:T(8,128)(2,1)} %all-gather.7.cloned.1.call-done, bf16[4096,1024]{0,1:T(8,128)(2,1)} %get-tuple-element.527, bf16[4096,1024]{0,1:T(8,128)(2,1)} %get-tuple-element.526), kind=kOutput, calls=%fused_computation.73 | convolution fusion | flops 34397487104 | bytes 41943040 | tf_op jit(solution)/shard_map/dot_general | solution.py:243
  988.5 508.7 %while.48 = (s32[]{:T(128)}, f32[2,2048,4,64]{3,2,1,0:T(4,128)}, f32[2,2048,4,64]{1,0,3,2:T(2,128)}, bf16[2,2048,4,64]{1,3,2,0:T(8,128)(2,1)}, s32[2]{0:T(128)S(...) while((s32[]{:T(128)}, f32[2,2048,4,64]{3,2,1,0:T(4,128)}, ...), condition=%wide.region_14.15_spmd, body=%wide.region_10.14_spmd.sunk | while | flops 2753165824 | bytes 271215808 | solution.py:165
  997.2 195.8 %while.49 = (s32[]{:T(128)}, f32[2048,4,64]{0,2,1:T(8,128)}, f32[2048,4,64]{0,2,1:T(8,128)}, f32[4,512,4,64]{1,3,2,0:T(8,128)}, s32[4]{0:T(128)S(1)}, /*index=5*...) while((s32[]{:T(128)}, f32[2048,4,64]{0,2,1:T(8,128)}, ...), condition=%wide.region_13.13_spmd.clone, body=%wide.region_11.12_spmd.clone.sunk | while | flops 2753165824 | bytes 197798400 | solution.py:160
  1196.7 35.8 %dynamic_update_slice.48 = f32[2,2048,4,64]{1,0,3,2:T(2,128)} dynamic-update-slice(f32[2,2048,4,64]{1,0,3,2:T(2,128)} %get-tuple-element.933, f32[1,2048,4,64]{1,0,3,2:T(1,128)S(1)} %copy.68, s32[]{:T(128)S(6)} %copy.103, s32[]{:T(128)} %constant.248.clone.1..sunk.1, s32[]{:T(128)} %constant.248.clone.1..sunk.1, s32[]{:T(128)} %constant.248.clone.1..sunk.1) | dynamic-update-slice | bytes 4194308 | tf_op jit(solution)/shard_map/while/body/jit(dynamic_update_index_in_dim)/dynamic_update_slice | solution.py:165
  1251.3 195.8 %while.49 = (s32[]{:T(128)}, f32[2048,4,64]{0,2,1:T(8,128)}, f32[2048,4,64]{0,2,1:T(8,128)}, f32[4,512,4,64]{1,3,2,0:T(8,128)}, s32[4]{0:T(128)S(1)}, /*index=5*...) while((s32[]{:T(128)}, f32[2048,4,64]{0,2,1:T(8,128)}, ...), condition=%wide.region_13.13_spmd.clone, body=%wide.region_11.12_spmd.clone.sunk | while | flops 2753165824 | bytes 197798400 | solution.py:160
  1450.8 35.8 %dynamic_update_slice.48 = f32[2,2048,4,64]{1,0,3,2:T(2,128)} dynamic-update-slice(f32[2,2048,4,64]{1,0,3,2:T(2,128)} %get-tuple-element.933, f32[1,2048,4,64]{1,0,3,2:T(1,128)S(1)} %copy.68, s32[]{:T(128)S(6)} %copy.103, s32[]{:T(128)} %constant.248.clone.1..sunk.1, s32[]{:T(128)} %constant.248.clone.1..sunk.1, s32[]{:T(128)} %constant.248.clone.1..sunk.1) | dynamic-update-slice | bytes 4194308 | tf_op jit(solution)/shard_map/while/body/jit(dynamic_update_index_in_dim)/dynamic_update_slice | solution.py:165
  1573.2 18.9 convolution_convert_fusion.6
  1592.1 19.8 convolution_convert_fusion
  1612.1 25.2 %convolution_convert_fusion.1 = bf16[4096,2048]{1,0:T(8,128)(2,1)} fusion(bf16[4096,1024]{0,1:T(8,128)(2,1)} %get-tuple-element.528, bf16[1024,2048]{1,0:T(8,128)(2,1)} %param.28), kind=kOutput, calls=%fused_computation.69 | convolution fusion | flops 17188257792 | bytes 29360128 | tf_op jit(solution)/shard_map/dot_general | solution.py:224
  1637.3 517.2 %all-reduce.4.cloned.1.call-done = (bf16[2048,768]{1,0:T(8,128)(2,1)}, bf16[256,2048]{1,0:T(8,128)(2,1)}, bf16[2048,2048]{1,0:T(8,128)(2,1)}, bf16[1024,2048]{1,0:T(8,128)(2,1)}) async-done(((bf16[2048,768]{1,0:T(8,128)(2,1)}, bf16[256,2048]{1,0:T(8,128)(2,1)}, bf16[2048,2048]{1,0:T(8,128)(2,1)}, bf16[1024,2048]{1,0:T(8,128)(2,1)}), (bf16[2048,768]{1,0:T(8,128)(2,1)}, bf16[256,2048]{1,0:T(8,128)(2,1)}, ...) | async-done | bytes 16777232 | tf_op jit(solution)/shard_map/psum | solution.py:293
  2183.6 89.6 %reduce-scatter.11.cloned.1.call-done = bf16[512,2048]{1,0:T(8,128)(2,1)} async-done(((bf16[4096,2048]{1,0:T(8,128)(2,1)}), bf16[512,2048]{1,0:T(8,128)(2,1)}) %reduce-scatter.11.cloned.1.call-update) | async-done | bytes 2097168 | tf_op jit(solution)/shard_map/reduce_scatter | solution.py:282
  2276.1 39.5 %all-reduce = (f32[2048]{0:T(1024)S(1)}, f32[2048]{0:T(1024)S(1)}) all-reduce(f32[2048]{0:T(1024)S(1)} %get-tuple-element.446, f32[2048]{0:T(1024)S(1)} %copy-done.43), channel_id=1, replica_groups=mesh['dp'=4,'tensor'=8] {'dp','tensor'}, use_global_device_ids=true, to_apply=%region_18.19 | all-reduce | flops 4096 | bytes 32768 | tf_op jit(solution)/shard_map/psum | solution.py:298
  2317.0 76.2 %reduce-scatter.7.cloned.1.call-done = bf16[512,2048]{1,0:T(8,128)(2,1)} async-done(((bf16[4096,2048]{1,0:T(8,128)(2,1)}), bf16[512,2048]{1,0:T(8,128)(2,1)}) %reduce-scatter.7.cloned.1.call-update) | async-done | bytes 2097168 | tf_op jit(solution)/shard_map/reduce_scatter | solution.py:223
  (475 shorter events, 843.9 us)
Async XLA Ops:
  7.2 357.8 %copy-start = (bf16[256,2048]{1,0:T(8,128)(2,1)S(1)}, bf16[256,2048]{1,0:T(8,128)(2,1)}, u32[]{:S(2)}) copy-start(bf16[256,2048]{1,0:T(8,128)(2,1)} %param.24) | copy-start | bytes 3145732
  7.2 99.0 %all-gather.5.cloned.1.call-start = ((), (), s32[]{:S(2)}) async-start(), calls=%async_computation.4 | async-start | bytes 18874368 | tf_op jit(solution)/shard_map/all_gather | solution.py:206
  13.6 477.5 %reduce-scatter.5.cloned.1.call-start = ((), (), s32[]{:S(2)}) async-start(), calls=%async_computation.5 | async-start | bytes 18874368 | tf_op jit(solution)/shard_map/reduce_scatter | solution.py:211
  374.7 116.4 %copy-start.7 = (bf16[512,2048]{1,0:T(8,128)(2,1)S(1)}, bf16[512,2048]{1,0:T(8,128)(2,1)}, u32[]{:S(2)}) copy-start(bf16[512,2048]{1,0:T(8,128)(2,1)} %param.19) | copy-start | bytes 6291460
  374.8 119.5 %copy-start.33 = (f32[2048]{0:T(1024)S(1)}, f32[2048]{0:T(1024)}, u32[]{:S(2)}) copy-start(f32[2048]{0:T(1024)} %param.25) | copy-start | bytes 24580
  374.8 211.7 %all-gather.7.cloned.1.call-start = ((), (), s32[]{:S(2)}) async-start(), calls=%async_computation.6 | async-start | bytes 18874368 | tf_op jit(solution)/shard_map/all_gather | solution.py:219
  496.6 181.4 %all-gather.9.cloned.1.call-start = ((), (), s32[]{:S(2)}) async-start(), calls=%async_computation.8 | async-start | bytes 18874368 | tf_op jit(solution)/shard_map/all_gather | solution.py:231
  497.2 375.4 %reduce-scatter.9.cloned.1.call-start = ((), (), s32[]{:S(2)}) async-start(), calls=%async_computation.9 | async-start | bytes 18874368 | tf_op jit(solution)/shard_map/reduce_scatter | solution.py:247
  756.2 116.4 %copy-start.8 = (bf16[512,2048]{1,0:T(8,128)(2,1)S(1)}, bf16[512,2048]{1,0:T(8,128)(2,1)}, u32[]{:S(2)}) copy-start(bf16[512,2048]{1,0:T(8,128)(2,1)} %param.19) | copy-start | bytes 6291460
  756.2 116.4 %copy-start.34 = (f32[2048]{0:T(1024)S(1)}, f32[2048]{0:T(1024)}, u32[]{:S(2)}) copy-start(f32[2048]{0:T(1024)} %param.25) | copy-start | bytes 24580
  756.2 116.4 %copy-start.39 = (f32[512]{0:T(512)S(1)}, f32[512]{0:T(512)}, u32[]{:S(2)}) copy-start(f32[512]{0:T(512)} %copy-done.38) | copy-start | bytes 6148
  756.2 215.1 %all-gather.11.cloned.1.call-start = ((), (), s32[]{:S(2)}) async-start(), calls=%async_computation.10 | async-start | bytes 18874368 | tf_op jit(solution)/shard_map/all_gather | solution.py:260
  881.5 1273.0 %all-reduce.4.cloned.1.call-start = ((), (), s32[]{:S(2)}) async-start(), calls=%async_computation.12 | async-start | bytes 33554432 | tf_op jit(solution)/shard_map/psum | solution.py:293
  1561.2 12.0 copy-start.26
  1561.2 12.0 copy-start.27
  1592.1 681.1 %reduce-scatter.11.cloned.1.call-start = ((), (), s32[]{:S(2)}) async-start(), calls=%async_computation.11 | async-start | bytes 18874368 | tf_op jit(solution)/shard_map/reduce_scatter | solution.py:282
  1612.0 781.1 %reduce-scatter.7.cloned.1.call-start = ((), (), s32[]{:S(2)}) async-start(), calls=%async_computation.7 | async-start | bytes 18874368 | tf_op jit(solution)/shard_map/reduce_scatter | solution.py:223
  2167.9 105.3 %copy-start.9 = (bf16[512,2048]{1,0:T(8,128)(2,1)S(1)}, bf16[512,2048]{1,0:T(8,128)(2,1)}, u32[]{:S(2)}) copy-start(bf16[512,2048]{1,0:T(8,128)(2,1)} %param.19) | copy-start | bytes 6291460
  2167.9 105.3 %copy-start.36 = (f32[2048]{0:T(1024)S(1)}, f32[2048]{0:T(1024)}, u32[]{:S(2)}) copy-start(f32[2048]{0:T(1024)} %param.20) | copy-start | bytes 24580
  2167.9 105.3 %copy-start.42 = (f32[512]{0:T(512)S(1)}, f32[512]{0:T(512)}, u32[]{:S(2)}) copy-start(f32[512]{0:T(512)} %copy-done.41) | copy-start | bytes 6148
  2183.5 92.6 %copy-start.43 = (f32[2048]{0:T(1024)S(1)}, f32[2048]{0:T(1024)}, u32[]{:S(2)}) copy-start(f32[2048]{0:T(1024)} %get-tuple-element.444) | copy-start | bytes 24580
  2183.6 209.6 %copy-start.35 = (f32[2048]{0:T(1024)S(1)}, f32[2048]{0:T(1024)}, u32[]{:S(2)}) copy-start(f32[2048]{0:T(1024)} %param.25) | copy-start | bytes 24580
  2183.6 209.6 %copy-start.40 = (f32[512]{0:T(512)S(1)}, f32[512]{0:T(512)}, u32[]{:S(2)}) copy-start(f32[512]{0:T(512)} %copy-done.38) | copy-start | bytes 6148
  2183.6 209.6 %copy-start.45 = (f32[512]{0:T(512)S(1)}, f32[512]{0:T(512)}, u32[]{:S(2)}) copy-start(f32[512]{0:T(512)} %copy-done.44) | copy-start | bytes 6148
  (85 other events, 454.8 us)
Sparse Core Ops, SparseCore 0:
  13.8 92.4 all-gather.4
  374.9 116.1 reduce-scatter.4
  496.7 89.7 all-gather.6
  588.2 89.7 all-gather.8
  756.4 116.1 reduce-scatter.8
  881.6 89.7 all-gather.10
  1592.2 562.2 all-reduce.3
  2158.1 115.1 reduce-scatter.10
  2276.8 116.3 reduce-scatter.6
where the time goes:
time: 2430 us; the launch traced here: 2410 us
  waiting for transfers between devices  1140 us (47%)
  matrix products  661 us (27%)
  local copies, waits for them, and re-layouts  296 us (12%)
  other arithmetic  218 us (9%)
  blocking collectives  39.5 us (2%)
  loops' own time  38.3 us (2%)
    psum x1, waiting for transfers between devices, local(): lax.psum(grad_joined.astype(jnp.bfloat16), 'dp').astype(jnp.float32)  517 us
    reduce_scatter x1, waiting for transfers between devices, local(): lax.psum_scatter(lax.dot_general(rows_here, both_w, (((1,), (1,)), ((), (...  116 us
    reduce_scatter x1, waiting for transfers between devices, local(): lax.psum_scatter(jnp.dot(attended, w_out, preferred_element_type=jnp.floa...  116 us
    dot_general x8, matrix products, one_step(): jnp.einsum('qhd,khd->hqk', grad_block, value_row, preferred_element_type=...  91.3 us
    reduce_scatter x1, waiting for transfers between devices, local(): lax.psum_scatter(lax.dot_general(rows_here, joined_w, (((1,), (1,)), ((),...  89.6 us
    dynamic_update_slice x8, local copies, waits for them, and re-layouts, attend_backward(): lax.map(one_row, jnp.arange(row_count, dtype=jnp.int32))  89.2 us
    all_gather x1, waiting for transfers between devices, local(): gathered_two = lax.all_gather(normed_two, 'tensor', axis=0, tiled=True)  81.7 us
    all_gather x1, waiting for transfers between devices, local(): gathered_one = lax.all_gather(normed_one, 'tensor', axis=0, tiled=True)  79.2 us
  transfers between devices with their start and end apart: 9, of which 9 were waited for; matrix products, arithmetic and copies ran while one was open for 9% of the time, Pallas kernels for 0%

commit v1 on v0

--- a/solution.py
+++ b/solution.py
@@ -290,7 +290,7 @@
     gain_one_part = jnp.sum(d_normed_one * unit_one, axis=0)
     input_grad = d_residual + norm_back(d_normed_one, gain_attn, unit_one, inverse_one)
     summed_joined, summed_outw, summed_both, summed_down = (
-        lax.psum(grad_joined.astype(jnp.bfloat16), "dp").astype(jnp.float32),
+        jnp.sum(lax.all_gather(grad_joined.astype(jnp.bfloat16), "dp"), axis=0).astype(jnp.float32),
         lax.psum(d_outw.astype(jnp.bfloat16), "dp").astype(jnp.float32),
         lax.psum(grad_both.astype(jnp.bfloat16), "dp").astype(jnp.float32),
         lax.psum(d_down.astype(jnp.bfloat16), "dp").astype(jnp.float32),

time: 2430 us -> 2190 us (0.901)
  waiting for transfers between devices: 1140 us -> 788 us
  matrix products: 661 us -> 768 us
    psum x1, waiting for transfers between devices: 517 us -> 0.02 us  [local(): lax.psum(d_outw.astype(jnp.bfloat16), 'dp').astype(jnp.float32)]
    all_gather x0 -> x1, waiting for transfers between devices: none -> 153 us  [local(): lax.all_gather(grad_joined.astype(jnp.bfloat16), 'dp')]
    dot_general x8, matrix products: 60.2 us -> 98.7 us  [one_step(): jnp.einsum('hqk,qhd->khd', probabilities.astype(jnp.bfloat16), grad_block...]
    dot_general x16, matrix products: 71.8 us -> 107 us  [block_scores(): jnp.einsum('qhd,khd->hqk', query_block, key_row, preferred_element_type=j...]
    dot_general x8, matrix products: 91.3 us -> 126 us  [one_step(): jnp.einsum('qhd,khd->hqk', grad_block, value_row, preferred_element_type=...]
    dot_general x8, matrix products: 22.9 us -> 56.4 us  [one_step(): jnp.einsum('hqk,qhd->khd', d_scores, query_block, preferred_element_type=...]
    dot_general x8, matrix products: 61.1 us -> 27.7 us  [one_step(): jnp.einsum('hqk,khd->qhd', d_scores, key_row, preferred_element_type=jnp....]
  transfers between devices with their start and end apart: 9 -> 10, of which waited for: 9 -> 9; matrix products, arithmetic and copies ran while one was open for 9% -> 41% of each run, Pallas kernels for 0% -> 0%
where the time goes in v1:
time: 2190 us; the launch traced here: 2170 us
  waiting for transfers between devices  788 us (36%)
  matrix products  768 us (35%)
  local copies, waits for them, and re-layouts  278 us (13%)
  other arithmetic  241 us (11%)
  blocking collectives  39.5 us (2%)
  loops' own time  38.4 us (2%)
    all_gather x1, waiting for transfers between devices, local(): lax.all_gather(grad_joined.astype(jnp.bfloat16), 'dp')  153 us
    dot_general x8, matrix products, one_step(): jnp.einsum('qhd,khd->hqk', grad_block, value_row, preferred_element_type=...  126 us
    reduce_scatter x1, waiting for transfers between devices, local(): lax.psum_scatter(lax.dot_general(rows_here, both_w, (((1,), (1,)), ((), (...  116 us
    reduce_scatter x1, waiting for transfers between devices, local(): lax.psum_scatter(jnp.dot(attended, w_out, preferred_element_type=jnp.floa...  116 us
    dot_general x16, matrix products, block_scores(): jnp.einsum('qhd,khd->hqk', query_block, key_row, preferred_element_type=j...  107 us
    reduce_scatter x1, waiting for transfers between devices, local(): lax.psum_scatter(lax.dot_general(rows_here, joined_w, (((1,), (1,)), ((),...  103 us
    dot_general x8, matrix products, one_step(): jnp.einsum('hqk,qhd->khd', probabilities.astype(jnp.bfloat16), grad_block...  98.7 us
    dynamic_update_slice x8, local copies, waits for them, and re-layouts, attend_backward(): lax.map(one_row, jnp.arange(row_count, dtype=jnp.int32))  89.2 us
  transfers between devices with their start and end apart: 10, of which 9 were waited for; matrix products, arithmetic and copies ran while one was open for 41% of the time, Pallas kernels for 0%

profile of v1, /device:TPU:0, one launch (start us, length us, event | category | flops | bytes accessed | tf_op | source)
XLA Modules:
  0.0 2169.0 jit_solution(8127480997387076564)
XLA Ops:
  27.1 79.2 %all-gather.7.cloned.1.call-done = bf16[4096,2048]{1,0:T(8,128)(2,1)} async-done(((bf16[512,2048]{1,0:T(8,128)(2,1)}), bf16[4096,2048]{1,0:T(8,128)(2,1)}) %all-gather.7.cloned.1.call-update) | async-done | bytes 16777232 | tf_op jit(solution)/shard_map/all_gather | solution.py:206
  106.2 20.4 fusion.84
  193.8 163.8 %while.46 = (s32[]{:T(128)}, bf16[8,512,4,64]{1,3,2,0:T(8,128)(2,1)}, f32[8,4,512]{2,1,0:T(4,128)}, s32[8]{0:T(128)S(1)}, bf16[2,2048,4,64]{1,3,2,0:T(8,128)(2,1...) while((s32[]{:T(128)}, ...), condition=%wide.region_4.5_spmd, body=%wide.region_1.4_spmd.sunk | while | flops 1127348736 | bytes 65637900 | solution.py:103
  373.6 115.8 %reduce-scatter.5.cloned.1.call-done = bf16[512,2048]{1,0:T(8,128)(2,1)} async-done(((bf16[4096,2048]{1,0:T(8,128)(2,1)}), bf16[512,2048]{1,0:T(8,128)(2,1)}) %reduce-scatter.5.cloned.1.call-update) | async-done | bytes 2097168 | tf_op jit(solution)/shard_map/reduce_scatter | solution.py:211
  503.0 81.7 %all-gather.9.cloned.1.call-done = bf16[4096,2048]{1,0:T(8,128)(2,1)} async-done(((bf16[512,2048]{1,0:T(8,128)(2,1)}), bf16[4096,2048]{1,0:T(8,128)(2,1)}) %all-gather.9.cloned.1.call-update) | async-done | bytes 16777232 | tf_op jit(solution)/shard_map/all_gather | solution.py:219
  584.8 44.9 %fusion.85 = f32[4096,2048]{0,1:T(8,128)} fusion(bf16[4096,2048]{1,0:T(8,128)(2,1)} %all-gather.9.cloned.1.call-done, bf16[2048,2048]{1,0:T(8,128)(2,1)} %constant_dynamic-update-slice_fusion.3), kind=kOutput, calls=%fused_computation.157 | convolution fusion | flops 34359738368 | bytes 58720256 | tf_op jit(solution)/shard_map/dot_general | solution.py:175
  629.7 46.6 %all-gather.11.cloned.1.call-done = bf16[4096,2048]{1,0:T(8,128)(2,1)} async-done(((bf16[512,2048]{1,0:T(8,128)(2,1)}), bf16[4096,2048]{1,0:T(8,128)(2,1)}) %all-gather.11.cloned.1.call-update) | async-done | bytes 16777232 | tf_op jit(solution)/shard_map/all_gather | solution.py:231
  676.3 36.1 %multiply_convert_fusion.2 = (bf16[4096,1024]{0,1:T(8,128)(2,1)}, bf16[4096,1024]{0,1:T(8,128)(2,1)}, bf16[4096,1024]{0,1:T(8,128)(2,1)}) fusion(f32[4096,2048]{0,1:T(8,128)} %fusion.85, bf16[4096,2048]{1,0:T(8,128)(2,1)} %all-gather.11.cloned.1.call-done, bf16[1024,2048]{1,0:T(8,128)(2,1)} %param.28), kind=kOutput, calls=%fused_computation.64 | convolution fusion | flops 17242783744 | bytes 79691776 | tf_op jit(solution)/shard_map/dot_general | solution.py:235
  712.4 42.1 %convolution_convert_fusion.3 = bf16[4096,2048]{1,0:T(8,128)(2,1)} fusion(bf16[2048,2048]{1,0:T(8,128)(2,1)} %constant_dynamic-update-slice_fusion.3, bf16[4096,1024]{0,1:T(8,128)(2,1)} %get-tuple-element.526, bf16[4096,1024]{0,1:T(8,128)(2,1)} %get-tuple-element.525), kind=kOutput, calls=%fused_computation.71 | convolution fusion | flops 34401681408 | bytes 41943040 | tf_op jit(solution)/shard_map/dot_general | solution.py:248
  755.0 115.9 %reduce-scatter.9.cloned.1.call-done = bf16[512,2048]{1,0:T(8,128)(2,1)} async-done(((bf16[4096,2048]{1,0:T(8,128)(2,1)}), bf16[512,2048]{1,0:T(8,128)(2,1)}) %reduce-scatter.9.cloned.1.call-update) | async-done | bytes 2097168 | tf_op jit(solution)/shard_map/reduce_scatter | solution.py:247
  883.3 24.7 %convolution_convert_fusion.5 = bf16[1024,2048]{1,0:T(8,128)(2,1)} fusion(bf16[4096,1024]{0,1:T(8,128)(2,1)} %get-tuple-element.527, bf16[4096,2048]{1,0:T(8,128)(2,1)} %all-gather.11.cloned.1.call-done), kind=kOutput, calls=%fused_computation.117 | convolution fusion | flops 17181966336 | bytes 29360128 | tf_op jit(solution)/shard_map/dot_general | solution.py:232
  907.9 45.2 %fusion.47 = bf16[2048,2048]{1,0:T(8,128)(2,1)} fusion(bf16[4096,2048]{1,0:T(8,128)(2,1)} %all-gather.9.cloned.1.call-done, bf16[4096,1024]{0,1:T(8,128)(2,1)} %get-tuple-element.526, bf16[4096,1024]{0,1:T(8,128)(2,1)} %get-tuple-element.525), kind=kOutput, calls=%fused_computation.73 | convolution fusion | flops 34397487104 | bytes 41943040 | tf_op jit(solution)/shard_map/dot_general | solution.py:243
  997.6 620.2 %while.48 = (s32[]{:T(128)}, f32[2,2048,4,64]{3,2,1,0:T(4,128)}, f32[2,2048,4,64]{1,0,3,2:T(2,128)}, bf16[2,2048,4,64]{1,3,2,0:T(8,128)(2,1)}, s32[2]{0:T(128)S(...) while((s32[]{:T(128)}, f32[2,2048,4,64]{3,2,1,0:T(4,128)}, ...), condition=%wide.region_14.15_spmd, body=%wide.region_10.14_spmd.sunk | while | flops 2753165824 | bytes 302674656 | solution.py:165
  1006.6 252.4 %while.49 = (s32[]{:T(128)}, f32[2048,4,64]{0,2,1:T(8,128)}, f32[2048,4,64]{0,2,1:T(8,128)}, f32[4,512,4,64]{1,3,2,0:T(8,128)}, s32[4]{0:T(128)S(1)}, /*index=5*...) while((s32[]{:T(128)}, f32[2048,4,64]{0,2,1:T(8,128)}, ...), condition=%wide.region_13.13_spmd.clone, body=%wide.region_11.12_spmd.clone.sunk | while | flops 2753165824 | bytes 243936352 | solution.py:160
  1269.8 35.9 %dynamic_update_slice.48 = f32[2,2048,4,64]{1,0,3,2:T(2,128)} dynamic-update-slice(f32[2,2048,4,64]{1,0,3,2:T(2,128)} %get-tuple-element.932, f32[1,2048,4,64]{1,0,3,2:T(1,128)S(1)} %copy.68, s32[]{:T(128)} %get-tuple-element.930, s32[]{:T(128)} %constant.249.clone.1..sunk.1, s32[]{:T(128)} %constant.249.clone.1..sunk.1, s32[]{:T(128)} %constant.249.clone.1..sunk.1) | dynamic-update-slice | bytes 4194308 | tf_op jit(solution)/shard_map/while/body/jit(dynamic_update_index_in_dim)/dynamic_update_slice | solution.py:165
  1316.7 251.6 %while.49 = (s32[]{:T(128)}, f32[2048,4,64]{0,2,1:T(8,128)}, f32[2048,4,64]{0,2,1:T(8,128)}, f32[4,512,4,64]{1,3,2,0:T(8,128)}, s32[4]{0:T(128)S(1)}, /*index=5*...) while((s32[]{:T(128)}, f32[2048,4,64]{0,2,1:T(8,128)}, ...), condition=%wide.region_13.13_spmd.clone, body=%wide.region_11.12_spmd.clone.sunk | while | flops 2753165824 | bytes 243936352 | solution.py:160
  1579.1 35.8 %dynamic_update_slice.48 = f32[2,2048,4,64]{1,0,3,2:T(2,128)} dynamic-update-slice(f32[2,2048,4,64]{1,0,3,2:T(2,128)} %get-tuple-element.932, f32[1,2048,4,64]{1,0,3,2:T(1,128)S(1)} %copy.68, s32[]{:T(128)} %get-tuple-element.930, s32[]{:T(128)} %constant.249.clone.1..sunk.1, s32[]{:T(128)} %constant.249.clone.1..sunk.1, s32[]{:T(128)} %constant.249.clone.1..sunk.1) | dynamic-update-slice | bytes 4194308 | tf_op jit(solution)/shard_map/while/body/jit(dynamic_update_index_in_dim)/dynamic_update_slice | solution.py:165
  1676.7 21.2 convolution_convert_fusion.6
  1697.9 20.0 convolution_convert_fusion
  1718.0 25.0 %convolution_convert_fusion.1 = bf16[4096,2048]{1,0:T(8,128)(2,1)} fusion(bf16[4096,1024]{0,1:T(8,128)(2,1)} %get-tuple-element.527, bf16[1024,2048]{1,0:T(8,128)(2,1)} %param.28), kind=kOutput, calls=%fused_computation.69 | convolution fusion | flops 17188257792 | bytes 29360128 | tf_op jit(solution)/shard_map/dot_general | solution.py:224
  1763.2 153.0 %all-gather.15.cloned.1.call-done = bf16[8192,768]{1,0:T(8,128)(2,1)} async-done(((bf16[2048,768]{1,0:T(8,128)(2,1)}), bf16[8192,768]{1,0:T(8,128)(2,1)}) %all-gather.15.cloned.1.call-update) | async-done | bytes 12582928 | tf_op jit(solution)/shard_map/all_gather | solution.py:293
  1931.4 102.8 %reduce-scatter.11.cloned.1.call-done = bf16[512,2048]{1,0:T(8,128)(2,1)} async-done(((bf16[4096,2048]{1,0:T(8,128)(2,1)}), bf16[512,2048]{1,0:T(8,128)(2,1)}) %reduce-scatter.11.cloned.1.call-update) | async-done | bytes 2097168 | tf_op jit(solution)/shard_map/reduce_scatter | solution.py:282
  2037.1 39.5 %all-reduce = (f32[2048]{0:T(1024)S(1)}, f32[2048]{0:T(1024)S(1)}) all-reduce(f32[2048]{0:T(1024)S(1)} %get-tuple-element.446, f32[2048]{0:T(1024)S(1)} %copy-done.46), channel_id=1, replica_groups=mesh['dp'=4,'tensor'=8] {'dp','tensor'}, use_global_device_ids=true, to_apply=%region_18.19 | all-reduce | flops 4096 | bytes 32768 | tf_op jit(solution)/shard_map/psum | solution.py:298
  2077.9 76.1 %reduce-scatter.7.cloned.1.call-done = bf16[512,2048]{1,0:T(8,128)(2,1)} async-done(((bf16[4096,2048]{1,0:T(8,128)(2,1)}), bf16[512,2048]{1,0:T(8,128)(2,1)}) %reduce-scatter.7.cloned.1.call-update) | async-done | bytes 2097168 | tf_op jit(solution)/shard_map/reduce_scatter | solution.py:223
  (581 shorter events, 954.0 us)
Async XLA Ops:
  7.2 356.1 %copy-start = (bf16[256,2048]{1,0:T(8,128)(2,1)S(1)}, bf16[256,2048]{1,0:T(8,128)(2,1)}, u32[]{:S(2)}) copy-start(bf16[256,2048]{1,0:T(8,128)(2,1)} %param.24) | copy-start | bytes 3145732
  7.2 99.0 %all-gather.7.cloned.1.call-start = ((), (), s32[]{:S(2)}) async-start(), calls=%async_computation.4 | async-start | bytes 18874368 | tf_op jit(solution)/shard_map/all_gather | solution.py:206
  13.6 475.8 %reduce-scatter.5.cloned.1.call-start = ((), (), s32[]{:S(2)}) async-start(), calls=%async_computation.5 | async-start | bytes 18874368 | tf_op jit(solution)/shard_map/reduce_scatter | solution.py:211
  373.0 116.4 %copy-start.8 = (bf16[512,2048]{1,0:T(8,128)(2,1)S(1)}, bf16[512,2048]{1,0:T(8,128)(2,1)}, u32[]{:S(2)}) copy-start(bf16[512,2048]{1,0:T(8,128)(2,1)} %param.19) | copy-start | bytes 6291460
  373.1 119.4 %copy-start.36 = (f32[2048]{0:T(1024)S(1)}, f32[2048]{0:T(1024)}, u32[]{:S(2)}) copy-start(f32[2048]{0:T(1024)} %param.25) | copy-start | bytes 24580
  373.1 211.7 %all-gather.9.cloned.1.call-start = ((), (), s32[]{:S(2)}) async-start(), calls=%async_computation.6 | async-start | bytes 18874368 | tf_op jit(solution)/shard_map/all_gather | solution.py:219
  494.9 181.4 %all-gather.11.cloned.1.call-start = ((), (), s32[]{:S(2)}) async-start(), calls=%async_computation.8 | async-start | bytes 18874368 | tf_op jit(solution)/shard_map/all_gather | solution.py:231
  495.5 375.4 %reduce-scatter.9.cloned.1.call-start = ((), (), s32[]{:S(2)}) async-start(), calls=%async_computation.9 | async-start | bytes 18874368 | tf_op jit(solution)/shard_map/reduce_scatter | solution.py:247
  754.5 116.4 %copy-start.9 = (bf16[512,2048]{1,0:T(8,128)(2,1)S(1)}, bf16[512,2048]{1,0:T(8,128)(2,1)}, u32[]{:S(2)}) copy-start(bf16[512,2048]{1,0:T(8,128)(2,1)} %param.19) | copy-start | bytes 6291460
  754.5 116.4 %copy-start.37 = (f32[2048]{0:T(1024)S(1)}, f32[2048]{0:T(1024)}, u32[]{:S(2)}) copy-start(f32[2048]{0:T(1024)} %param.25) | copy-start | bytes 24580
  754.5 116.4 %copy-start.42 = (f32[512]{0:T(512)S(1)}, f32[512]{0:T(512)}, u32[]{:S(2)}) copy-start(f32[512]{0:T(512)} %copy-done.41) | copy-start | bytes 6148
  754.5 215.1 %all-gather.13.cloned.1.call-start = ((), (), s32[]{:S(2)}) async-start(), calls=%async_computation.10 | async-start | bytes 18874368 | tf_op jit(solution)/shard_map/all_gather | solution.py:260
  879.7 863.3 %all-reduce.4.cloned.1.call-start = ((), (), s32[]{:S(2)}) async-start(), calls=%async_computation.13 | async-start | bytes 27262976 | tf_op jit(solution)/shard_map/psum | solution.py:294
  997.5 918.6 %all-gather.15.cloned.1.call-start = ((), (), s32[]{:S(2)}) async-start(), calls=%async_computation.12 | async-start | bytes 15728640 | tf_op jit(solution)/shard_map/all_gather | solution.py:293
  1269.8 38.6 %copy-start.53 = (s32[2]{0:T(128)S(1)}, s32[2]{0:T(128)}, u32[]{:S(2)}) copy-start(s32[2]{0:T(128)} %copy-done.52) | copy-start | bytes 28 | tf_op jit(solution)/shard_map/while
  1697.9 336.3 %reduce-scatter.11.cloned.1.call-start = ((), (), s32[]{:S(2)}) async-start(), calls=%async_computation.11 | async-start | bytes 18874368 | tf_op jit(solution)/shard_map/reduce_scatter | solution.py:282
  1717.9 436.0 %reduce-scatter.7.cloned.1.call-start = ((), (), s32[]{:S(2)}) async-start(), calls=%async_computation.7 | async-start | bytes 18874368 | tf_op jit(solution)/shard_map/reduce_scatter | solution.py:223
  1925.1 109.0 %copy-start.10 = (bf16[512,2048]{1,0:T(8,128)(2,1)S(1)}, bf16[512,2048]{1,0:T(8,128)(2,1)}, u32[]{:S(2)}) copy-start(bf16[512,2048]{1,0:T(8,128)(2,1)} %param.19) | copy-start | bytes 6291460
  1925.1 109.0 %copy-start.39 = (f32[2048]{0:T(1024)S(1)}, f32[2048]{0:T(1024)}, u32[]{:S(2)}) copy-start(f32[2048]{0:T(1024)} %param.20) | copy-start | bytes 24580
  1925.1 109.0 %copy-start.45 = (f32[512]{0:T(512)S(1)}, f32[512]{0:T(512)}, u32[]{:S(2)}) copy-start(f32[512]{0:T(512)} %copy-done.44) | copy-start | bytes 6148
  1931.4 105.7 %copy-start.46 = (f32[2048]{0:T(1024)S(1)}, f32[2048]{0:T(1024)}, u32[]{:S(2)}) copy-start(f32[2048]{0:T(1024)} %get-tuple-element.444) | copy-start | bytes 24580
  1931.4 222.5 %copy-start.38 = (f32[2048]{0:T(1024)S(1)}, f32[2048]{0:T(1024)}, u32[]{:S(2)}) copy-start(f32[2048]{0:T(1024)} %param.25) | copy-start | bytes 24580
  1931.4 222.5 %copy-start.43 = (f32[512]{0:T(512)S(1)}, f32[512]{0:T(512)}, u32[]{:S(2)}) copy-start(f32[512]{0:T(512)} %copy-done.41) | copy-start | bytes 6148
  1931.4 222.5 %copy-start.48 = (f32[512]{0:T(512)S(1)}, f32[512]{0:T(512)}, u32[]{:S(2)}) copy-start(f32[512]{0:T(512)} %copy-done.47) | copy-start | bytes 6148
  (133 other events, 1354.1 us)
Sparse Core Ops, SparseCore 0:
  13.7 92.4 all-gather.6
  373.2 116.1 reduce-scatter.4
  495.0 89.7 all-gather.8
  586.5 89.7 all-gather.10
  754.6 116.1 reduce-scatter.8
  879.9 89.7 all-gather.12
  997.6 459.9 all-reduce.3
  1698.0 218.1 all-gather.14
  1919.7 114.3 reduce-scatter.10
  2037.6 116.3 reduce-scatter.6
